TPU v7x, 32 devices: a whole 2x2x4 slice. The times are simulated.
32 devices in a mesh: band: 8 (over y, x, core), gslab: 4 (over z).
Axes of the slice: x: 2, y: 2, z: 4, core: 2. Of those that a mesh axis runs over, the one named last changes fastest.
Arguments:
- band_coeffs: float32 [3072, 49152], P('band', 'gslab'), may hold values from -6 to 6
- sign_table: int32 [12, 3072], P(None, 'band'), may hold values from -1 to 1, as said below
- slice_widths: int32 [16], replicated, may hold values from 96 to 384, as said below
- owner_map: int32 [16], replicated, may hold values from 0 to 15, each once
Outputs:
- pseudobands: float32 [192, 49152], P(('band', 'gslab'))
Inputs may be any that keep to these rules, and one draw needn't show every extreme that they name: `sign_table`: every entry is -1 or 1. `slice_widths`: the widths sum to 3072; every slice holds 96 to 384 bands, and in every draw some slice holds exactly 96 and some exactly 384. `owner_map`: each slice appears once.
All inputs are finite; a program needn't handle non-finite values.
Results may differ from a plain program's by a relative error of at most 0.0003.
Values sent between devices are 32-bit elements; how exact they have to be, the bound alone decides.
A program may use at most 128 MiB of HBM per device.

v0:
```python
import jax
import jax.numpy as jnp
from jax import lax
from jax.sharding import PartitionSpec as P


def mixing_rows(row_ids, slice_of_band, sign_float, owner_map, inverse, per_slice):
    slice_count = owner_map.shape[0]
    slot_group = row_ids // per_slice
    within = row_ids % per_slice
    slice_range = jnp.arange(slice_count, dtype=jnp.int32)
    picked = slot_group[:, None] == slice_range[None, :]
    target = jnp.sum(jnp.where(picked, owner_map[None, :], 0), axis=1)
    member = target[:, None] == slice_range[None, :]
    row_scale = jnp.sum(jnp.where(member, inverse[None, :], 0.0), axis=1)
    one_hot = (within[:, None] == jnp.arange(per_slice, dtype=jnp.int32)[None, :]).astype(
        jnp.float32
    )
    sign_rows = jnp.dot(
        one_hot, sign_float, precision=lax.Precision.HIGHEST, preferred_element_type=jnp.float32
    )
    return jnp.where(slice_of_band[None, :] == target[:, None], sign_rows * row_scale[:, None], 0.0)


def on_device(band_coeffs, sign_table, slice_widths, owner_map):
    local_bands = band_coeffs.shape[0]
    per_slice = sign_table.shape[0]
    slice_count = owner_map.shape[0]
    total_rows = slice_count * per_slice
    band_groups = lax.axis_size("band")
    first_band = lax.axis_index("band") * local_bands
    band_ids = first_band + jnp.arange(local_bands, dtype=jnp.int32)
    ends = jnp.cumsum(slice_widths)
    slice_of_band = jnp.sum((band_ids[:, None] >= ends[None, :]).astype(jnp.int32), axis=1)
    inverse = 1.0 / jnp.sqrt(slice_widths.astype(jnp.float32))
    sign_float = sign_table.astype(jnp.float32)
    group_rows = total_rows // band_groups
    row_ids = jnp.arange(group_rows * lax.axis_size("band"), dtype=jnp.int32)
    mixing = mixing_rows(row_ids, slice_of_band, sign_float, owner_map, inverse, per_slice)
    summed = lax.psum_scatter(
        jnp.dot(
            mixing, band_coeffs, precision=lax.Precision.HIGHEST, preferred_element_type=jnp.float32
        ),
        "band",
        scatter_dimension=0,
        tiled=True,
    )
    return lax.all_to_all(summed, "gslab", split_axis=0, concat_axis=1, tiled=True)


def solution(mesh):
    return jax.shard_map(
        on_device,
        mesh=mesh,
        in_specs=(P("band", "gslab"), P(None, "band"), P(), P()),
        out_specs=P(("band", "gslab"), None),
        check_vma=False,
    )
```

profile of v0, /device:TPU:0, one launch (start us, length us, event | category | flops | bytes accessed | tf_op | source)
XLA Modules:
  0.0 161.3 jit_solution(13425090234396967158)
XLA Ops:
  6.5 0.0 reduce-scatter.2.cloned.1.call-start
  6.6 0.7 convert_rsqrt_fusion
  7.2 0.7 copy.7
  8.0 0.1 reduce
  8.1 0.7 select_reduce_fusion.1
  8.9 0.1 select_reduce_fusion
  9.0 0.1 convert_reduce_fusion
  9.0 1.1 fusion
  10.1 20.8 %fusion.5 = f32[192,12288]{1,0:T(8,128)} fusion(f32[192,384]{1,0:T(8,128)S(1)} %fusion, f32[384,12288]{1,0:T(8,128)} %param.4), kind=kOutput, calls=%fused_computation.19 | convolution fusion | flops 10871635968 | bytes 28606464 | tf_op jit(solution)/shard_map/dot_general | solution.py:41
  31.0 0.0 reduce-scatter.2.cloned.1.call-update
  31.0 79.7 %reduce-scatter.2.cloned.1.call-done = f32[24,12288]{1,0:T(8,128)} async-done(((f32[192,12288]{1,0:T(8,128)}), f32[24,12288]{1,0:T(8,128)}) %reduce-scatter.2.cloned.1.call-update) | async-done | bytes 1179664 | tf_op jit(solution)/shard_map/reduce_scatter | solution.py:40
  110.7 1.4 all_to_all.14
  112.1 41.2 %all_to_all.19 = f32[4,6,12288]{2,1,0:T(8,128)S(1)} all-to-all(f32[4,6,12288]{2,1,0:T(8,128)S(1)} %all_to_all.14), channel_id=1, replica_groups=mesh['band'=8,'gslab'=4] {'gslab'}, dimensions={0} | all-to-all | bytes 2359296 | tf_op jit(solution)/shard_map/all_to_all | solution.py:48
  153.3 1.1 copy.9
  (4 shorter events, 0.1 us)
Async XLA Ops:
  6.5 104.1 %reduce-scatter.2.cloned.1.call-start = ((), (), s32[]{:S(2)}) async-start(), calls=%async_computation.2 | async-start | bytes 10616832 | tf_op jit(solution)/shard_map/reduce_scatter | solution.py:40
Sparse Core Ops, SparseCore 0:
  31.1 79.5 reduce-scatter.1
where the time goes:
time: 162 us; the launch traced here: 161 us
  waiting for transfers between devices  79.7 us (49%)
  blocking collectives  41.2 us (25%)
  matrix products  21.9 us (14%)
  between operations  13.4 us (8%)
  local copies, waits for them, and re-layouts  3.3 us (2%)
  other arithmetic  1.76 us (1%)
    reduce_scatter x1, waiting for transfers between devices, on_device(): lax.psum_scatter(jnp.dot(mixing, band_coeffs, precision=lax.Precision.HIG...  79.7 us
    all_to_all x1, blocking collectives, on_device(): lax.all_to_all(summed, 'gslab', split_axis=0, concat_axis=1, tiled=True)  41.2 us
    dot_general x1, matrix products, on_device(): jnp.dot(mixing, band_coeffs, precision=lax.Precision.HIGHEST, preferred_e...  20.8 us
  transfers between devices with their start and end apart: 1, of which 1 were waited for; matrix products, arithmetic and copies ran while one was open for 0% of the time, Pallas kernels for 0%

commit v1 on v0

--- a/solution.py
+++ b/solution.py
@@ -1,7 +1,16 @@
+import functools
+
 import jax
 import jax.numpy as jnp
 from jax import lax
+from jax.experimental import pallas as pl
+from jax.experimental.pallas import tpu as pltpu
 from jax.sharding import PartitionSpec as P
+
+NARROWEST = 96
+LANES = 128
+AHEAD = 4
+MESH = pl.DeviceIdType.MESH
 
 
 def mixing_rows(row_ids, slice_of_band, sign_float, owner_map, inverse, per_slice):
@@ -22,20 +31,18 @@
     return jnp.where(slice_of_band[None, :] == target[:, None], sign_rows * row_scale[:, None], 0.0)
 
 
-def on_device(band_coeffs, sign_table, slice_widths, owner_map):
+def dense(band_coeffs, sign_table, slice_widths, owner_map):
     local_bands = band_coeffs.shape[0]
     per_slice = sign_table.shape[0]
     slice_count = owner_map.shape[0]
     total_rows = slice_count * per_slice
-    band_groups = lax.axis_size("band")
     first_band = lax.axis_index("band") * local_bands
     band_ids = first_band + jnp.arange(local_bands, dtype=jnp.int32)
     ends = jnp.cumsum(slice_widths)
     slice_of_band = jnp.sum((band_ids[:, None] >= ends[None, :]).astype(jnp.int32), axis=1)
     inverse = 1.0 / jnp.sqrt(slice_widths.astype(jnp.float32))
     sign_float = sign_table.astype(jnp.float32)
-    group_rows = total_rows // band_groups
-    row_ids = jnp.arange(group_rows * lax.axis_size("band"), dtype=jnp.int32)
+    row_ids = jnp.arange(total_rows, dtype=jnp.int32)
     mixing = mixing_rows(row_ids, slice_of_band, sign_float, owner_map, inverse, per_slice)
     summed = lax.psum_scatter(
         jnp.dot(
@@ -48,9 +55,234 @@
     return lax.all_to_all(summed, "gslab", split_axis=0, concat_axis=1, tiled=True)
 
 
+def two_term_dot(exact, values):
+    high = values.astype(jnp.bfloat16)
+    low = (values - high.astype(jnp.float32)).astype(jnp.bfloat16)
+    return jnp.dot(exact, high, preferred_element_type=jnp.float32) + jnp.dot(
+        exact, low, preferred_element_type=jnp.float32
+    )
+
+
+def kernel(
+    groups, slabs, pieces, reach,
+    widths_ref, owner_ref, signs_ref, band_ref, out_ref,
+    held, mix, sent, got, chosen, scale, done,
+    load_sem, send1, recv1, send2, recv2,
+):
+    devices = groups * slabs
+    my_group = lax.axis_index("band")
+    my_slab = lax.axis_index("gslab")
+    me = my_group * slabs + my_slab
+    per_slice, local_bands = signs_ref.shape
+    slices = widths_ref.shape[0]
+    packed, width = sent.shape[2:]
+    mine = done.shape[2]
+    slot = chosen.shape[0] // devices
+    total = groups * pieces
+
+    def load(step):
+        part = step // groups
+        group = lax.rem(my_group + 1 + lax.rem(step, groups), groups)
+        index = group * pieces + part
+        return pltpu.make_async_copy(
+            band_ref.at[:, pl.ds(pl.multiple_of(index * width, width), width)],
+            held.at[index],
+            load_sem.at[index],
+        )
+
+    for step in range(AHEAD):
+        load(step).start()
+
+    barrier = pltpu.get_barrier_semaphore()
+
+    @pl.loop(1, devices)
+    def _(k):
+        other = lax.rem(me + k, devices)
+        pl.semaphore_signal(
+            barrier, inc=1,
+            device_id={"band": other // slabs, "gslab": lax.rem(other, slabs)},
+            device_id_type=MESH,
+        )
+
+    ends = []
+    running = jnp.int32(0)
+    for s in range(slices):
+        running = running + widths_ref[s]
+        ends.append(running)
+
+    first_band = my_group * local_bands
+    bands = first_band + lax.broadcasted_iota(jnp.int32, (1, local_bands), 1)
+    slice_of = jnp.zeros((1, local_bands), jnp.int32)
+    first = jnp.int32(0)
+    for s in range(slices):
+        slice_of = slice_of + jnp.where(bands >= ends[s], 1, 0)
+        first = first + jnp.where(first_band >= ends[s], 1, 0)
+    row = lax.broadcasted_iota(jnp.int32, (packed, per_slice), 0)
+    column = lax.broadcasted_iota(jnp.int32, (packed, per_slice), 1)
+    repeat = jnp.where(lax.rem(row, per_slice) == column, 1.0, 0.0).astype(jnp.float32)
+    signs = jnp.dot(
+        repeat, signs_ref[...].astype(jnp.float32), preferred_element_type=jnp.float32
+    )
+    row = lax.broadcasted_iota(jnp.int32, (packed, local_bands), 0)
+    hit = (slice_of - first == row // per_slice) & (row < reach * per_slice)
+    mix[...] = jnp.where(hit, signs, 0.0).astype(jnp.bfloat16)
+
+    def exchange(group, source, part):
+        return pltpu.make_async_remote_copy(
+            src_ref=sent.at[part, group],
+            dst_ref=got.at[part, source],
+            send_sem=send1.at[part, group],
+            recv_sem=recv1.at[part, source],
+            device_id={"band": group, "gslab": my_slab},
+            device_id_type=MESH,
+        )
+
+    def partial_sums(part, k):
+        step = part * groups + k
+        load(step).wait()
+
+        @pl.when(step + AHEAD < total)
+        def _():
+            load(step + AHEAD).start()
+
+        group = lax.rem(my_group + 1 + k, groups)
+        return group, two_term_dot(mix[...], held[group * pieces + part])
+
+    def send_partial(part):
+        @pl.loop(0, groups - 1)
+        def _(k):
+            group, value = partial_sums(part, k)
+            sent[part, group] = value
+            exchange(group, my_group, part).start()
+
+        _, value = partial_sums(part, groups - 1)
+        got[part, my_group] = value
+
+    def columns(group, slab, part):
+        start = slab * (total * width) + (group * pieces + part) * width
+        return out_ref.at[:, pl.ds(pl.multiple_of(start, width), width)]
+
+    def deliver(other, source, part):
+        return pltpu.make_async_remote_copy(
+            src_ref=done.at[part, other],
+            dst_ref=columns(source // slabs, lax.rem(source, slabs), part),
+            send_sem=send2.at[part, other],
+            recv_sem=recv2.at[part, source],
+            device_id={"band": other // slabs, "gslab": lax.rem(other, slabs)},
+            device_id_type=MESH,
+        )
+
+    def keep(part):
+        return pltpu.make_async_copy(
+            done.at[part, me], columns(my_group, my_slab, part), recv2.at[part, me]
+        )
+
+    def finish(part):
+        @pl.loop(1, groups)
+        def _(k):
+            source = lax.rem(my_group + k, groups)
+            exchange(source, source, part).wait_recv()
+
+        rows = got[part].reshape(groups * packed, width)
+        value = two_term_dot(chosen[...], rows) * scale[:, :1]
+        done[part] = value.reshape(devices, slot, width)[:, :mine]
+        keep(part).start()
+
+        @pl.loop(1, devices)
+        def _(k):
+            deliver(lax.rem(me + k, devices), me, part).start()
+
+    pl.semaphore_wait(barrier, devices - 1)
+    send_partial(0)
+
+    shape = (devices * slot, 1)
+    tall = lax.broadcasted_iota(jnp.int32, shape, 0)
+    within = lax.rem(tall, slot)
+    output_row = (tall // slot) * mine + within
+    block = output_row // per_slice
+    target = jnp.zeros(shape, jnp.int32)
+    for s in range(slices):
+        target = jnp.where(block == s, owner_ref[s], target)
+    breadth = jnp.ones(shape, jnp.int32)
+    for s in range(slices):
+        breadth = jnp.where(target == s, widths_ref[s], breadth)
+    scale[...] = jnp.broadcast_to(1.0 / jnp.sqrt(breadth.astype(jnp.float32)), scale.shape)
+    wanted = jnp.where(within < mine, target * per_slice + lax.rem(output_row, per_slice), -1)
+    wide = lax.broadcasted_iota(jnp.int32, (1, groups * packed), 1)
+    place = lax.rem(wide, packed)
+    begin = (wide // packed) * local_bands
+    lowest = jnp.zeros((1, groups * packed), jnp.int32)
+    for s in range(slices):
+        lowest = lowest + jnp.where(begin >= ends[s], 1, 0)
+    offered = jnp.where(place < reach * per_slice, lowest * per_slice + place, -2)
+    chosen[...] = jnp.where(wanted == offered, 1.0, 0.0).astype(jnp.bfloat16)
+
+    for part in range(1, pieces):
+        send_partial(part)
+        finish(part - 1)
+    finish(pieces - 1)
+
+    for part in range(pieces):
+        @pl.loop(1, groups)
+        def _(k):
+            exchange(lax.rem(my_group + k, groups), my_group, part).wait_send()
+
+        @pl.loop(1, devices)
+        def _(k):
+            other = lax.rem(me + k, devices)
+            deliver(other, other, part).wait()
+
+        keep(part).wait()
+
+
+def on_device(groups, slabs, band_coeffs, sign_table, slice_widths, owner_map):
+    local_bands, local_columns = band_coeffs.shape
+    per_slice = sign_table.shape[0]
+    rows = owner_map.shape[0] * per_slice
+    devices = groups * slabs
+    share, odd = divmod(local_columns, groups * LANES)
+    if odd or rows % devices:
+        return dense(band_coeffs, sign_table, slice_widths, owner_map)
+    pieces = next(p for p in (3, 4, 2, 1) if share % p == 0)
+    width = share // pieces * LANES
+    reach = (local_bands - 2) // NARROWEST + 2
+    packed = -(-reach * per_slice // 8) * 8
+    mine = rows // devices
+    slot = -(-mine // 8) * 8
+    return pl.pallas_call(
+        functools.partial(kernel, groups, slabs, pieces, reach),
+        out_shape=jax.ShapeDtypeStruct((mine, local_columns * slabs), jnp.float32),
+        in_specs=[
+            pl.BlockSpec(memory_space=pltpu.SMEM),
+            pl.BlockSpec(memory_space=pltpu.SMEM),
+            pl.BlockSpec(memory_space=pltpu.VMEM),
+            pl.BlockSpec(memory_space=pl.ANY),
+        ],
+        out_specs=pl.BlockSpec(memory_space=pl.ANY),
+        scratch_shapes=[
+            pltpu.VMEM((groups * pieces, local_bands, width), jnp.float32),
+            pltpu.VMEM((packed, local_bands), jnp.bfloat16),
+            pltpu.VMEM((pieces, groups, packed, width), jnp.float32),
+            pltpu.VMEM((pieces, groups, packed, width), jnp.float32),
+            pltpu.VMEM((devices * slot, groups * packed), jnp.bfloat16),
+            pltpu.VMEM((devices * slot, LANES), jnp.float32),
+            pltpu.VMEM((pieces, devices, mine, width), jnp.float32),
+            pltpu.SemaphoreType.DMA((groups * pieces,)),
+            pltpu.SemaphoreType.DMA((pieces, groups)),
+            pltpu.SemaphoreType.DMA((pieces, groups)),
+            pltpu.SemaphoreType.DMA((pieces, devices)),
+            pltpu.SemaphoreType.DMA((pieces, devices)),
+        ],
+        compiler_params=pltpu.CompilerParams(
+            collective_id=0, has_side_effects=True, vmem_limit_bytes=56 * 2**20
+        ),
+        name="pseudobands",
+    )(slice_widths, owner_map, sign_table, band_coeffs)
+
+
 def solution(mesh):
     return jax.shard_map(
-        on_device,
+        functools.partial(on_device, mesh.shape["band"], mesh.shape["gslab"]),
         mesh=mesh,
         in_specs=(P("band", "gslab"), P(None, "band"), P(), P()),
         out_specs=P(("band", "gslab"), None),

time: 162 us -> 71.7 us (0.44)
  waiting for transfers between devices: 79.7 us -> 0 us
  Pallas kernels: 0 us -> 68.8 us
  blocking collectives: 41.2 us -> 0 us
  matrix products: 21.9 us -> 0 us
  between operations: 13.4 us -> 0.01 us
  other arithmetic: 1.76 us -> 0 us
    reduce_scatter x1 -> x0, waiting for transfers between devices: 79.7 us -> none  [on_device(): lax.psum_scatter(jnp.dot(mixing, band_coeffs, precision=lax.Precision.HIG...]
    pallas_call x0 -> x1, Pallas kernels: none -> 68.8 us  [on_device(): pl.pallas_call(functools.partial(kernel, groups, slabs, pieces, reach), o...]
    all_to_all x1 -> x0, blocking collectives: 41.2 us -> none  [on_device(): lax.all_to_all(summed, 'gslab', split_axis=0, concat_axis=1, tiled=True)]
    dot_general x2 -> x0, matrix products: 21.9 us -> none  [the longest x1 20.8 us: on_device(): jnp.dot(mixing, band_coeffs, precision=lax.Precision.HIGHEST, preferred_e...]
  transfers between devices with their start and end apart: 1 -> 0, of which waited for: 1 -> 0; matrix products, arithmetic and copies ran while one was open for 0% -> 0% of each run, Pallas kernels for 0% -> 0%
where the time goes in v1:
time: 71.7 us; the launch traced here: 71.4 us
  Pallas kernels  68.8 us (96%)
  local copies, waits for them, and re-layouts  2.65 us (4%)
    pallas_call x1, Pallas kernels, on_device(): pl.pallas_call(functools.partial(kernel, groups, slabs, pieces, reach), o...  68.8 us
    unnamed x1, local copies, waits for them, and re-layouts  2.65 us

profile of v1, /device:TPU:0, one launch (start us, length us, event | category | flops | bytes accessed | tf_op | source)
XLA Modules:
  0.0 71.4 jit_solution(2415554473187320300)
XLA Ops:
  0.0 68.8 %pseudobands.1 = f32[6,49152]{1,0:T(8,128)} custom-call(s32[16]{0:T(128)} %widths_ref.1, s32[16]{0:T(128)} %owner_ref.1, s32[12,384]{1,0:T(8,128)} %signs_ref.1, f32[384,12288]{1,0:T(8,128)} %band_ref.1), custom_call_target="tpu_custom_call" | custom-call | tf_op jit(solution)/shard_map/pseudobands/pallas_call | solution.py:252
  68.8 2.7 %copy.6 = f32[6,49152]{1,0:T(8,128)} copy(f32[6,49152]{1,0:T(8,128)} %pseudobands.1) | data formatting | bytes 2359296

commit v2 on v1

v2 whole, which is shorter than its diff:
```python
import functools

import jax
import jax.numpy as jnp
from jax import lax
from jax.experimental import pallas as pl
from jax.experimental.pallas import tpu as pltpu
from jax.sharding import PartitionSpec as P

NARROWEST = 96
LANES = 128
PIECES = (8, 4, 2, 1)
MERGE_LAG = 2
FINISH_LAG = 4
MESH = pl.DeviceIdType.MESH


def mixing_rows(row_ids, slice_of_band, sign_float, owner_map, inverse, per_slice):
    slice_count = owner_map.shape[0]
    slot_group = row_ids // per_slice
    within = row_ids % per_slice
    slice_range = jnp.arange(slice_count, dtype=jnp.int32)
    picked = slot_group[:, None] == slice_range[None, :]
    target = jnp.sum(jnp.where(picked, owner_map[None, :], 0), axis=1)
    member = target[:, None] == slice_range[None, :]
    row_scale = jnp.sum(jnp.where(member, inverse[None, :], 0.0), axis=1)
    one_hot = (within[:, None] == jnp.arange(per_slice, dtype=jnp.int32)[None, :]).astype(
        jnp.float32
    )
    sign_rows = jnp.dot(
        one_hot, sign_float, precision=lax.Precision.HIGHEST, preferred_element_type=jnp.float32
    )
    return jnp.where(slice_of_band[None, :] == target[:, None], sign_rows * row_scale[:, None], 0.0)


def dense(band_coeffs, sign_table, slice_widths, owner_map):
    local_bands = band_coeffs.shape[0]
    per_slice = sign_table.shape[0]
    slice_count = owner_map.shape[0]
    total_rows = slice_count * per_slice
    first_band = lax.axis_index("band") * local_bands
    band_ids = first_band + jnp.arange(local_bands, dtype=jnp.int32)
    ends = jnp.cumsum(slice_widths)
    slice_of_band = jnp.sum((band_ids[:, None] >= ends[None, :]).astype(jnp.int32), axis=1)
    inverse = 1.0 / jnp.sqrt(slice_widths.astype(jnp.float32))
    sign_float = sign_table.astype(jnp.float32)
    row_ids = jnp.arange(total_rows, dtype=jnp.int32)
    mixing = mixing_rows(row_ids, slice_of_band, sign_float, owner_map, inverse, per_slice)
    summed = lax.psum_scatter(
        jnp.dot(
            mixing, band_coeffs, precision=lax.Precision.HIGHEST, preferred_element_type=jnp.float32
        ),
        "band",
        scatter_dimension=0,
        tiled=True,
    )
    return lax.all_to_all(summed, "gslab", split_axis=0, concat_axis=1, tiled=True)


def two_term_dot(exact, values):
    high = values.astype(jnp.bfloat16)
    low = (values - high.astype(jnp.float32)).astype(jnp.bfloat16)
    return jnp.dot(exact, high, preferred_element_type=jnp.float32) + jnp.dot(
        exact, low, preferred_element_type=jnp.float32
    )


def kernel(
    slabs, pieces, reach,
    widths_ref, owner_ref, signs_ref, band_ref, out_ref,
    held, mix, sent, got, chosen, scale, half, came, done,
    load_sem, send1, recv1, send2, recv2, send3, recv3,
):
    my_group = lax.axis_index("band")
    my_slab = lax.axis_index("gslab")
    my_core = lax.rem(my_group, 2)
    bits = (my_group // 4, lax.rem(my_group // 2, 2))
    devices = 8 * slabs
    me = my_group * slabs + my_slab
    per_slice, local_bands = signs_ref.shape
    slices = widths_ref.shape[0]
    packed, width = sent.shape[2:]
    mine = done.shape[2]
    peers = done.shape[1]
    live = reach * per_slice
    total = 4 * pieces

    def group_of(axis, along, other, core):
        return along * 4 + other * 2 + core if axis == 0 else other * 4 + along * 2 + core

    def own(axis):
        return bits[axis], bits[1 - axis]

    def quarter_at(axis, k):
        return lax.rem(own(axis)[0] * 2 + my_core + 1 + k, 4)

    def load(part, quarter):
        index = quarter * pieces + part
        return pltpu.make_async_copy(
            band_ref.at[:, pl.ds(pl.multiple_of(index * width, width), width)],
            held.at[index],
            load_sem.at[index],
        )

    def load_piece(part):
        for k in range(4):
            load(part, quarter_at(part % 2, k)).start()

    load_piece(0)
    barrier = pltpu.get_barrier_semaphore()

    @pl.loop(1, devices)
    def _(k):
        other = lax.rem(me + k, devices)
        pl.semaphore_signal(
            barrier, inc=1,
            device_id={"band": other // slabs, "gslab": lax.rem(other, slabs)},
            device_id_type=MESH,
        )

    ends = []
    running = jnp.int32(0)
    for s in range(slices):
        running = running + widths_ref[s]
        ends.append(running)

    first_band = my_group * local_bands
    bands = first_band + lax.broadcasted_iota(jnp.int32, (1, local_bands), 1)
    slice_of = jnp.zeros((1, local_bands), jnp.int32)
    first = jnp.int32(0)
    for s in range(slices):
        slice_of = slice_of + jnp.where(bands >= ends[s], 1, 0)
        first = first + jnp.where(first_band >= ends[s], 1, 0)
    row = lax.broadcasted_iota(jnp.int32, (packed, per_slice), 0)
    column = lax.broadcasted_iota(jnp.int32, (packed, per_slice), 1)
    repeat = jnp.where(lax.rem(row, per_slice) == column, 1.0, 0.0).astype(jnp.float32)
    signs = jnp.dot(
        repeat, signs_ref[...].astype(jnp.float32), preferred_element_type=jnp.float32
    )
    row = lax.broadcasted_iota(jnp.int32, (packed, local_bands), 0)
    hit = (slice_of - first == row // per_slice) & (row < live)
    mix[...] = jnp.where(hit, signs, 0.0).astype(jnp.bfloat16)

    def exchange(part, quarter, source):
        axis = part % 2
        return pltpu.make_async_remote_copy(
            src_ref=sent.at[part, quarter],
            dst_ref=got.at[part, source],
            send_sem=send1.at[part, quarter],
            recv_sem=recv1.at[part, source],
            device_id={
                "band": group_of(axis, quarter // 2, own(axis)[1], lax.rem(quarter, 2)),
                "gslab": my_slab,
            },
            device_id_type=MESH,
        )

    def partial_sums(part, quarter):
        load(part, quarter).wait()
        return two_term_dot(mix[...], held[quarter * pieces + part])

    def send_partial(part):
        if part + 1 < pieces:
            load_piece(part + 1)
        here = own(part % 2)[0] * 2 + my_core

        @pl.loop(0, 3)
        def _(k):
            quarter = quarter_at(part % 2, k)
            sent[part, quarter] = partial_sums(part, quarter)
            exchange(part, quarter, here).start()

        got[part, here] = partial_sums(part, here)

    def cross(part):
        axis = part % 2
        along, other = own(axis)
        return pltpu.make_async_remote_copy(
            src_ref=half.at[part, 0],
            dst_ref=came.at[part],
            send_sem=send2.at[part],
            recv_sem=recv2.at[part],
            device_id={"band": group_of(axis, along, 1 - other, my_core), "gslab": my_slab},
            device_id_type=MESH,
        )

    def merge(part):
        axis = part % 2

        @pl.loop(0, 3)
        def _(k):
            source = quarter_at(axis, k)
            exchange(part, source, source).wait_recv()

        rows = got[part].reshape(4 * packed, width)
        value = two_term_dot(chosen[axis], rows)
        half[part] = value.reshape(2, peers * mine, width)
        cross(part).start()

    def here_of(axis):
        return (own(axis)[0] * 2 + my_core) * slabs + my_slab

    def columns(part, peer):
        start = lax.rem(peer, slabs) * (total * width) + ((peer // slabs) * pieces + part) * width
        return out_ref.at[:, pl.ds(pl.multiple_of(start, width), width)]

    def deliver(part, peer, source):
        axis = part % 2
        quarter = peer // slabs
        return pltpu.make_async_remote_copy(
            src_ref=done.at[part, peer],
            dst_ref=columns(part, source),
            send_sem=send3.at[part, peer],
            recv_sem=recv3.at[part, source],
            device_id={
                "band": group_of(axis, quarter // 2, own(axis)[1], lax.rem(quarter, 2)),
                "gslab": lax.rem(peer, slabs),
            },
            device_id_type=MESH,
        )

    def keep(part):
        here = here_of(part % 2)
        return pltpu.make_async_copy(done.at[part, here], columns(part, here), recv3.at[part, here])

    def finish(part):
        axis = part % 2
        cross(part).wait_recv()
        for peer in range(peers):
            rows = slice(peer * mine, (peer + 1) * mine)
            done[part, peer] = (half[part, 1, rows] + came[part, rows]) * scale[axis, rows, :1]
        keep(part).start()
        here = here_of(axis)

        @pl.loop(1, peers)
        def _(k):
            deliver(part, lax.rem(here + k, peers), here).start()

    pl.semaphore_wait(barrier, devices - 1)
    send_partial(0)

    for axis in range(2):
        along, other = own(axis)
        shape = (2 * peers * mine, 1)
        tall = lax.broadcasted_iota(jnp.int32, shape, 0)
        stays = tall // (peers * mine)
        rest = lax.rem(tall, peers * mine)
        peer = rest // mine
        quarter = peer // slabs
        side = jnp.where(stays == 1, other, 1 - other)
        group = group_of(axis, quarter // 2, side, lax.rem(quarter, 2))
        output_row = (group * slabs + lax.rem(peer, slabs)) * mine + lax.rem(rest, mine)
        block = output_row // per_slice
        target = jnp.zeros(shape, jnp.int32)
        for s in range(slices):
            target = jnp.where(block == s, owner_ref[s], target)
        breadth = jnp.ones(shape, jnp.int32)
        for s in range(slices):
            breadth = jnp.where(target == s, widths_ref[s], breadth)
        root = 1.0 / jnp.sqrt(breadth.astype(jnp.float32))
        scale[axis] = jnp.broadcast_to(root[peers * mine:], (peers * mine, LANES))
        wanted = target * per_slice + lax.rem(output_row, per_slice)
        wide = lax.broadcasted_iota(jnp.int32, (1, 4 * packed), 1)
        place = lax.rem(wide, packed)
        quarter = wide // packed
        begin = group_of(axis, quarter // 2, other, lax.rem(quarter, 2)) * local_bands
        lowest = jnp.zeros((1, 4 * packed), jnp.int32)
        for s in range(slices):
            lowest = lowest + jnp.where(begin >= ends[s], 1, 0)
        offered = jnp.where(place < live, lowest * per_slice + place, -2)
        chosen[axis] = jnp.where(wanted == offered, 1.0, 0.0).astype(jnp.bfloat16)

    for step in range(1, pieces + FINISH_LAG):
        if step < pieces:
            send_partial(step)
        if 0 <= step - MERGE_LAG < pieces:
            merge(step - MERGE_LAG)
        if 0 <= step - FINISH_LAG < pieces:
            finish(step - FINISH_LAG)

    for part in range(pieces):
        cross(part).wait_send()
        here = own(part % 2)[0] * 2 + my_core

        @pl.loop(0, 3)
        def _(k):
            exchange(part, quarter_at(part % 2, k), here).wait_send()

        here = here_of(part % 2)

        @pl.loop(1, peers)
        def _(k):
            peer = lax.rem(here + k, peers)
            deliver(part, peer, peer).wait()

        keep(part).wait()


def on_device(groups, slabs, band_coeffs, sign_table, slice_widths, owner_map):
    local_bands, local_columns = band_coeffs.shape
    per_slice = sign_table.shape[0]
    rows = owner_map.shape[0] * per_slice
    share, odd = divmod(local_columns, 4 * LANES)
    if groups != 8 or odd or rows % (8 * slabs):
        return dense(band_coeffs, sign_table, slice_widths, owner_map)
    pieces = next(p for p in PIECES if share % p == 0)
    width = share // pieces * LANES
    reach = (local_bands - 2) // NARROWEST + 2
    packed = -(-reach * per_slice // 8) * 8
    mine = rows // (8 * slabs)
    peers = 4 * slabs
    return pl.pallas_call(
        functools.partial(kernel, slabs, pieces, reach),
        out_shape=jax.ShapeDtypeStruct((mine, local_columns * slabs), jnp.float32),
        in_specs=[
            pl.BlockSpec(memory_space=pltpu.SMEM),
            pl.BlockSpec(memory_space=pltpu.SMEM),
            pl.BlockSpec(memory_space=pltpu.VMEM),
            pl.BlockSpec(memory_space=pl.ANY),
        ],
        out_specs=pl.BlockSpec(memory_space=pl.ANY),
        scratch_shapes=[
            pltpu.VMEM((4 * pieces, local_bands, width), jnp.float32),
            pltpu.VMEM((packed, local_bands), jnp.bfloat16),
            pltpu.VMEM((pieces, 4, packed, width), jnp.float32),
            pltpu.VMEM((pieces, 4, packed, width), jnp.float32),
            pltpu.VMEM((2, 2 * peers * mine, 4 * packed), jnp.bfloat16),
            pltpu.VMEM((2, peers * mine, LANES), jnp.float32),
            pltpu.VMEM((pieces, 2, peers * mine, width), jnp.float32),
            pltpu.VMEM((pieces, peers * mine, width), jnp.float32),
            pltpu.VMEM((pieces, peers, mine, width), jnp.float32),
            pltpu.SemaphoreType.DMA((4 * pieces,)),
            pltpu.SemaphoreType.DMA((pieces, 4)),
            pltpu.SemaphoreType.DMA((pieces, 4)),
            pltpu.SemaphoreType.DMA((pieces,)),
            pltpu.SemaphoreType.DMA((pieces,)),
            pltpu.SemaphoreType.DMA((pieces, peers)),
            pltpu.SemaphoreType.DMA((pieces, peers)),
        ],
        compiler_params=pltpu.CompilerParams(
            collective_id=0, has_side_effects=True, vmem_limit_bytes=60 * 2**20
        ),
        name="pseudobands",
    )(slice_widths, owner_map, sign_table, band_coeffs)


def solution(mesh):
    return jax.shard_map(
        functools.partial(on_device, mesh.shape["band"], mesh.shape["gslab"]),
        mesh=mesh,
        in_specs=(P("band", "gslab"), P(None, "band"), P(), P()),
        out_specs=P(("band", "gslab"), None),
        check_vma=False,
    )
```

time: 71.7 us -> 61.7 us (0.86)
  Pallas kernels: 68.8 us -> 58.9 us
    pallas_call x1, Pallas kernels: 68.8 us -> 58.9 us  [on_device(): pl.pallas_call(functools.partial(kernel, slabs, pieces, reach), out_shape...]
where the time goes in v2:
time: 61.7 us; the launch traced here: 61.5 us
  Pallas kernels  58.9 us (95%)
  local copies, waits for them, and re-layouts  2.65 us (4%)
    pallas_call x1, Pallas kernels, on_device(): pl.pallas_call(functools.partial(kernel, slabs, pieces, reach), out_shape...  58.9 us
    unnamed x1, local copies, waits for them, and re-layouts  2.65 us

profile of v2, /device:TPU:0, one launch (start us, length us, event | category | flops | bytes accessed | tf_op | source)
XLA Modules:
  0.0 61.5 jit_solution(9005165780577675365)
XLA Ops:
  0.0 58.9 %pseudobands.1 = f32[6,49152]{1,0:T(8,128)} custom-call(s32[16]{0:T(128)} %widths_ref.1, s32[16]{0:T(128)} %owner_ref.1, s32[12,384]{1,0:T(8,128)} %signs_ref.1, f32[384,12288]{1,0:T(8,128)} %band_ref.1), custom_call_target="tpu_custom_call" | custom-call | tf_op jit(solution)/shard_map/pseudobands/pallas_call | solution.py:312
  58.9 2.7 %copy.6 = f32[6,49152]{1,0:T(8,128)} copy(f32[6,49152]{1,0:T(8,128)} %pseudobands.1) | data formatting | bytes 2359296
